TPU v7x, 32 devices: a whole 2x2x4 slice. The times are simulated.
32 devices in a mesh: brick: 16 (over z, y, core), chan: 2 (over x).
Axes of the slice: x: 2, y: 2, z: 4, core: 2. Of those that a mesh axis runs over, the one named last changes fastest.
Arguments:
- volume: bfloat16 [32, 16, 64, 256], P('brick', 'chan'), may hold values from -6 to 6
- first_weight: bfloat16 [3, 3, 3, 256, 256], replicated, may hold values from -0.078125 to 0.078125
- second_weight: bfloat16 [3, 3, 3, 256, 256], replicated, may hold values from -0.078125 to 0.078125
- coarse_weight: bfloat16 [3, 3, 3, 256, 512], P(None, None, None, None, 'chan'), may hold values from -0.078125 to 0.078125
- projection: bfloat16 [512, 256], P('chan'), may hold values from -0.25 to 0.25
Outputs:
- merged: bfloat16 [32, 16, 64, 256], P('brick', 'chan')
All inputs are finite; a program needn't handle non-finite values.
Results may differ from a plain program's by a relative error of at most 0.011.
Values may be sent and summed in bfloat16 or wider, within the bound.
No kernel may reach another device: no remote copies, remote signals or barrier semaphores. Data moves between devices by JAX's collectives and lax.ppermute only.
A program may use at most 64 MiB of HBM per device.

v0:
```python
import jax
import jax.numpy as jnp
from jax import lax
from jax.sharding import PartitionSpec as P


def extended(block, sides, width):
    for axis, dim in sides:
        count = lax.axis_size(axis)
        forward = [(i, i + 1) for i in range(count - 1)]
        backward = [(target, source) for source, target in forward]
        low = lax.ppermute(
            lax.slice_in_dim(block, block.shape[dim] - width, None, axis=dim), axis, forward
        )
        high = lax.ppermute(lax.slice_in_dim(block, 0, width, axis=dim), axis, backward)
        block = jnp.concatenate([low, block, high], axis=dim)
    return block


def convolve(padded, weight):
    rows_x = padded.shape[0] - 2
    rows_y = padded.shape[1] - 2
    rows_z = padded.shape[2] - 2
    inputs_count = padded.shape[3]
    outputs_count = weight.shape[4]
    total = jnp.zeros((rows_x * rows_y * rows_z, outputs_count), jnp.float32)
    for offset_x in range(3):
        for offset_y in range(3):
            for offset_z in range(3):
                window = padded[
                    offset_x : offset_x + rows_x,
                    offset_y : offset_y + rows_y,
                    offset_z : offset_z + rows_z,
                ]
                window = window.reshape(-1, inputs_count)
                total = total + jnp.dot(
                    window, weight[offset_x, offset_y, offset_z], preferred_element_type=jnp.float32
                )
    return total.reshape(rows_x, rows_y, rows_z, outputs_count)


def fine_layer(field, weight):
    padded = extended(field, (("brick", 0), ("chan", 1)), 1)
    padded = jnp.pad(padded, ((0, 0), (0, 0), (1, 1), (0, 0)))
    return jnp.maximum(convolve(padded, weight), 0.0).astype(jnp.bfloat16)


def shards(volume, first_weight, second_weight, coarse_weight, projection):
    layer_one = fine_layer(volume, first_weight)
    skipped = fine_layer(layer_one, second_weight)
    size_x, size_y, size_z, channels_in = skipped.shape
    blocks = skipped.astype(jnp.float32).reshape(
        size_x // 2, 2, size_y // 2, 2, size_z // 2, 2, channels_in
    )
    pooled = jnp.mean(blocks, axis=(1, 3, 5)).astype(jnp.bfloat16)
    brick_cells = lax.all_gather(pooled, "chan", axis=1, tiled=True)
    padded = extended(brick_cells, (("brick", 0),), 1)
    padded = jnp.pad(padded, ((0, 0), (1, 1), (1, 1), (0, 0)))
    coarse = jnp.maximum(convolve(padded, coarse_weight), 0.0).astype(jnp.bfloat16)
    own_cells = lax.all_to_all(coarse, "chan", split_axis=1, concat_axis=3, tiled=True)
    whole_projection = lax.all_gather(projection, "chan", axis=0, tiled=True)
    own_shape = own_cells.shape
    lifted = jnp.dot(
        own_cells.reshape(-1, own_shape[3]), whole_projection, preferred_element_type=jnp.float32
    )
    lifted = lifted.reshape(own_shape[0], own_shape[1], own_shape[2], channels_in)
    upsampled = jnp.repeat(jnp.repeat(jnp.repeat(lifted, 2, axis=0), 2, axis=1), 2, axis=2)
    return (skipped.astype(jnp.float32) + upsampled).astype(jnp.bfloat16)


def solution(mesh):
    in_specs = (
        P("brick", "chan", None, None),
        P(),
        P(),
        P(None, None, None, None, "chan"),
        P("chan", None),
    )
    out_specs = P("brick", "chan", None, None)
    return jax.shard_map(shards, mesh=mesh, in_specs=in_specs, out_specs=out_specs, check_vma=False)
```

profile of v0, /device:TPU:21, one launch (start us, length us, event | category | flops | bytes accessed | tf_op | source)
XLA Modules:
  0.0 105.2 jit_solution(181432394441561462)
XLA Ops:
  0.0 1.2 %fusion.277 = (bf16[1,8,64,256]{3,2,1,0:T(8,128)(2,1)S(1)}, bf16[1,8,64,256]{3,2,1,0:T(8,128)(2,1)S(1)}) fusion(bf16[2,8,64,256]{3,2,1,0:T(8,128)(2,1)} %param.5), kind=kLoop, calls=%fused_computation.343 | loop fusion | bytes 1048576 | tf_op jit(solution)/shard_map/slice | solution.py:15
  1.2 3.8 %collective-permute-start = (bf16[1,8,64,256]{3,2,1,0:T(8,128)(2,1)S(1)}, bf16[1,8,64,256]{3,2,1,0:T(8,128)(2,1)S(1)}, u32[]{:S(2)}, u32[]{:S(2)}) collective-permute-start(bf16[1,8,64,256]{3,2,1,0:T(8,128)(2,1)S(1)} %get-tuple-element.94), channel_id=1, source_target_pairs={{0,2},{2,4},{4,6},{6,8},{8,10},{10,12},{12,14},{14,16},{16,18},{18... | collective-permute-start | bytes 786440 | tf_op jit(solution)/shard_map/ppermute | solution.py:12
  5.1 1.9 %collective-permute-start.1 = (bf16[1,8,64,256]{3,2,1,0:T(8,128)(2,1)S(1)}, bf16[1,8,64,256]{3,2,1,0:T(8,128)(2,1)S(1)}, u32[]{:S(2)}, u32[]{:S(2)}) collective-permute-start(bf16[1,8,64,256]{3,2,1,0:T(8,128)(2,1)S(1)} %get-tuple-element.93), channel_id=1, source_target_pairs={{2,0},{4,2},{6,4},{8,6},{10,8},{12,10},{14,12},{16,14},{18,16},{20... | collective-permute-start | bytes 786440 | tf_op jit(solution)/shard_map/ppermute | solution.py:15
  7.0 1.4 %fusion.160 = f32[1024,256]{1,0:T(8,128)S(1)} fusion(bf16[1024,256]{1,0:T(8,128)(2,1)} %bitcast.426, bf16[3,3,3,256,256]{4,3,2,1,0:T(8,128)(2,1)} %param.6), kind=kOutput, calls=%fused_computation.221 | convolution fusion | flops 134217728 | bytes 1703936 | tf_op jit(solution)/shard_map/dot_general | solution.py:36
  8.4 5.3 %collective-permute-done.1 = bf16[1,8,64,256]{3,2,1,0:T(8,128)(2,1)S(1)} collective-permute-done((bf16[1,8,64,256]{3,2,1,0:T(8,128)(2,1)S(1)}, bf16[1,8,64,256]{3,2,1,0:T(8,128)(2,1)S(1)}, u32[]{:S(2)}, u32[]{:S(2)}) %collective-permute-start.1) | collective-permute-done | bytes 262176 | tf_op jit(solution)/shard_map/ppermute | solution.py:15
  13.9 3.1 %collective-permute-start.2 = (bf16[4,1,64,256]{3,2,1,0:T(8,128)(2,1)S(1)}, bf16[4,1,64,256]{3,2,1,0:T(8,128)(2,1)S(1)}, u32[]{:S(2)}, u32[]{:S(2)}) collective-permute-start(bf16[4,1,64,256]{3,2,1,0:T(8,128)(2,1)S(1)} %get-tuple-element.60), channel_id=1, source_target_pairs={{0,1},{2,3},{4,5},{6,7},{8,9},{10,11},{12,13},{14,15},{16,17},{18,... | collective-permute-start | bytes 393224 | tf_op jit(solution)/shard_map/ppermute | solution.py:12
  17.0 1.3 %collective-permute-start.3 = (bf16[4,1,64,256]{3,2,1,0:T(8,128)(2,1)S(1)}, bf16[4,1,64,256]{3,2,1,0:T(8,128)(2,1)S(1)}, u32[]{:S(2)}, u32[]{:S(2)}) collective-permute-start(bf16[4,1,64,256]{3,2,1,0:T(8,128)(2,1)S(1)} %get-tuple-element.61), channel_id=1, source_target_pairs={{1,0},{3,2},{5,4},{7,6},{9,8},{11,10},{13,12},{15,14},{17,16},{19,... | collective-permute-start | bytes 393224 | tf_op jit(solution)/shard_map/ppermute | solution.py:15
  19.0 3.8 %collective-permute-done.3 = bf16[4,1,64,256]{3,2,1,0:T(8,128)(2,1)S(1)} collective-permute-done((bf16[4,1,64,256]{3,2,1,0:T(8,128)(2,1)S(1)}, bf16[4,1,64,256]{3,2,1,0:T(8,128)(2,1)S(1)}, u32[]{:S(2)}, u32[]{:S(2)}) %collective-permute-start.3) | collective-permute-done | bytes 131104 | tf_op jit(solution)/shard_map/ppermute | solution.py:15
  22.8 0.8 fusion.8
  23.5 3.1 %fusion.270 = (bf16[2,8,64,256]{3,2,1,0:T(8,128)(2,1)S(1)}, bf16[2,8,64,256]{3,2,1,0:T(8,128)(2,1)S(1)}, bf16[2,8,64,256]{3,2,1,0:T(8,128)(2,1)S(1)}, bf16[2,8,6...) fusion(bf16[4,10,66,256]{3,2,1,0:T(8,128)(2,1)S(1)} %fusion.8), kind=kLoop, calls=%fused_computation.336 | loop fusion | bytes 18874368 | tf_op jit(solution)/shard_map/slice | solution.py:30
  33.5 1.3 %fusion.184 = f32[1024,256]{1,0:T(8,128)} fusion(bf16[1024,256]{1,0:T(8,128)(2,1)S(1)} %bitcast.466, bf16[3,3,3,256,256]{4,3,2,1,0:T(8,128)(2,1)S(1)} %copy-done.3), kind=kOutput, calls=%fused_computation.245 | convolution fusion | flops 134217728 | bytes 1703936 | tf_op jit(solution)/shard_map/dot_general | solution.py:36
  34.8 2.6 %fusion.40 = bf16[1024,256]{1,0:T(8,128)(2,1)S(1)} fusion(f32[1024,256]{1,0:T(8,128)S(1)} %fusion.135, f32[1024,256]{1,0:T(8,128)S(1)} %fusion.137, f32[1024,256]{1,0:T(8,128)S(1)} %fusion.139, f32[1024,256]{1,0:T(8,128)S(1)} %fusion.141, f32[1024,256]{1,0:T(8,128)S(1)} %fusion.143, f32[1024,256]{1,0:T(8,128)S(1)} %fusion.145, ...), kind=kOutput, calls=%fused_computation.59 | convolution fusion | flops 141557760 | bytes 28442624 | tf_op jit(solution)/shard_map/dot_general | solution.py:36
  37.5 4.5 %collective-permute-start.4 = (bf16[1,8,64,256]{3,2,1,0:T(8,128)(2,1)S(1)}, bf16[1,8,64,256]{3,2,1,0:T(8,128)(2,1)S(1)}, u32[]{:S(2)}, u32[]{:S(2)}) collective-permute-start(bf16[1,8,64,256]{3,2,1,0:T(8,128)(2,1)S(1)} %bitcast.513), channel_id=1, source_target_pairs={{0,2},{2,4},{4,6},{6,8},{8,10},{10,12},{12,14},{14,16},{16,18},{18... | collective-permute-start | bytes 786440 | tf_op jit(solution)/shard_map/ppermute | solution.py:12
  42.0 1.9 %collective-permute-start.5 = (bf16[1,8,64,256]{3,2,1,0:T(8,128)(2,1)S(1)}, bf16[1,8,64,256]{3,2,1,0:T(8,128)(2,1)S(1)}, u32[]{:S(2)}, u32[]{:S(2)}) collective-permute-start(bf16[1,8,64,256]{3,2,1,0:T(8,128)(2,1)S(1)} %bitcast.512), channel_id=1, source_target_pairs={{2,0},{4,2},{6,4},{8,6},{10,8},{12,10},{14,12},{16,14},{18,16},{20... | collective-permute-start | bytes 786440 | tf_op jit(solution)/shard_map/ppermute | solution.py:15
  43.9 1.2 %fusion.109 = f32[1024,256]{1,0:T(8,128)S(1)} fusion(bf16[1024,256]{1,0:T(8,128)(2,1)S(1)} %fusion.40, bf16[3,3,3,256,256]{4,3,2,1,0:T(8,128)(2,1)} %param.7), kind=kOutput, calls=%fused_computation.170 | convolution fusion | flops 134217728 | bytes 1703936 | tf_op jit(solution)/shard_map/dot_general | solution.py:36
  45.3 5.3 %collective-permute-done.5 = bf16[1,8,64,256]{3,2,1,0:T(8,128)(2,1)S(1)} collective-permute-done((bf16[1,8,64,256]{3,2,1,0:T(8,128)(2,1)S(1)}, bf16[1,8,64,256]{3,2,1,0:T(8,128)(2,1)S(1)}, u32[]{:S(2)}, u32[]{:S(2)}) %collective-permute-start.5) | collective-permute-done | bytes 262176 | tf_op jit(solution)/shard_map/ppermute | solution.py:15
  51.0 1.3 %collective-permute-start.6 = (bf16[4,1,64,256]{3,2,1,0:T(8,128)(2,1)S(1)}, bf16[4,1,64,256]{3,2,1,0:T(8,128)(2,1)S(1)}, u32[]{:S(2)}, u32[]{:S(2)}) collective-permute-start(bf16[4,1,64,256]{3,2,1,0:T(8,128)(2,1)S(1)} %get-tuple-element.55), channel_id=1, source_target_pairs={{0,1},{2,3},{4,5},{6,7},{8,9},{10,11},{12,13},{14,15},{16,17},{18,... | collective-permute-start | bytes 393224 | tf_op jit(solution)/shard_map/ppermute | solution.py:12
  52.3 1.5 %collective-permute-start.7 = (bf16[4,1,64,256]{3,2,1,0:T(8,128)(2,1)S(1)}, bf16[4,1,64,256]{3,2,1,0:T(8,128)(2,1)S(1)}, u32[]{:S(2)}, u32[]{:S(2)}) collective-permute-start(bf16[4,1,64,256]{3,2,1,0:T(8,128)(2,1)S(1)} %get-tuple-element.56), channel_id=1, source_target_pairs={{1,0},{3,2},{5,4},{7,6},{9,8},{11,10},{13,12},{15,14},{17,16},{19,... | collective-permute-start | bytes 393224 | tf_op jit(solution)/shard_map/ppermute | solution.py:15
  54.3 3.8 %collective-permute-done.7 = bf16[4,1,64,256]{3,2,1,0:T(8,128)(2,1)S(1)} collective-permute-done((bf16[4,1,64,256]{3,2,1,0:T(8,128)(2,1)S(1)}, bf16[4,1,64,256]{3,2,1,0:T(8,128)(2,1)S(1)}, u32[]{:S(2)}, u32[]{:S(2)}) %collective-permute-start.7) | collective-permute-done | bytes 131104 | tf_op jit(solution)/shard_map/ppermute | solution.py:15
  58.1 0.8 select_maximum_fusion
  58.9 3.3 %fusion.269 = (bf16[2,8,64,256]{3,2,1,0:T(8,128)(2,1)S(1)}, bf16[2,8,64,256]{3,2,1,0:T(8,128)(2,1)S(1)}, bf16[2,8,64,256]{3,2,1,0:T(8,128)(2,1)S(1)}, bf16[2,8,6...) fusion(bf16[4,10,66,256]{3,2,1,0:T(8,128)(2,1)S(1)} %select_max, ...), kind=kLoop, calls=%fused_computation.335 | loop fusion | bytes 18874368 | tf_op jit(solution)/shard_map/slice | solution.py:30
  68.1 0.8 fusion.24
  70.7 0.6 reshape.411
  71.3 0.5 reduce_sum.9
  71.9 4.0 %all-gather = bf16[8,32,256]{2,1,0:T(8,128)(2,1)S(1)} all-gather(bf16[4,32,256]{2,1,0:T(8,128)(2,1)S(1)} %multiply_convert_fusion), channel_id=2, replica_groups=mesh['brick'=16,'chan'=2] {'chan'}, dimensions={0}, use_global_device_ids=true | all-gather | bytes 196608 | tf_op jit(solution)/shard_map/all_gather | solution.py:56
  75.9 5.4 %collective-permute-start.8 = (bf16[1,8,32,256]{3,2,1,0:T(8,128)(2,1)S(1)}, bf16[1,8,32,256]{3,2,1,0:T(8,128)(2,1)S(1)}, u32[]{:S(2)}, u32[]{:S(2)}) collective-permute-start(bf16[1,8,32,256]{3,2,1,0:T(8,128)(2,1)S(1)} %bitcast.479), channel_id=1, source_target_pairs={{0,2},{2,4},{4,6},{6,8},{8,10},{10,12},{12,14},{14,16},{16,18},{18... | collective-permute-start | bytes 393224 | tf_op jit(solution)/shard_map/ppermute | solution.py:12
  81.3 1.9 %collective-permute-start.9 = (bf16[1,8,32,256]{3,2,1,0:T(8,128)(2,1)S(1)}, bf16[1,8,32,256]{3,2,1,0:T(8,128)(2,1)S(1)}, u32[]{:S(2)}, u32[]{:S(2)}) collective-permute-start(bf16[1,8,32,256]{3,2,1,0:T(8,128)(2,1)S(1)} %bitcast.480), channel_id=1, source_target_pairs={{2,0},{4,2},{6,4},{8,6},{10,8},{12,10},{14,12},{16,14},{18,16},{20... | collective-permute-start | bytes 393224 | tf_op jit(solution)/shard_map/ppermute | solution.py:15
  83.2 5.2 %collective-permute-done.9 = bf16[1,8,32,256]{3,2,1,0:T(8,128)(2,1)S(1)} collective-permute-done((bf16[1,8,32,256]{3,2,1,0:T(8,128)(2,1)S(1)}, bf16[1,8,32,256]{3,2,1,0:T(8,128)(2,1)S(1)}, u32[]{:S(2)}, u32[]{:S(2)}) %collective-permute-start.9) | collective-permute-done | bytes 131104 | tf_op jit(solution)/shard_map/ppermute | solution.py:15
  94.3 0.8 fusion.47
  95.1 3.4 %all-to-all-start = ((bf16[1,8,32,256]{3,2,0,1:T(8,128)(2,1)}), bf16[1,8,32,256]{3,2,0,1:T(8,128)(2,1)S(1)}, u32[]{:S(2)}, u32[]{:S(2)}) async-start(bf16[1,8,32,256]{3,2,0,1:T(8,128)(2,1)} %bitcast.167), calls=%async_computation | async-start | bytes 262144 | tf_op jit(solution)/shard_map/all_to_all | solution.py:60
  98.5 4.7 %all_gather.7 = bf16[512,256]{1,0:T(8,128)(2,1)S(1)} all-gather(bf16[256,256]{1,0:T(8,128)(2,1)S(1)} %copy-done.4), channel_id=1, replica_groups=mesh['brick'=16,'chan'=2] {'chan'}, dimensions={0}, use_global_device_ids=true | all-gather | bytes 393216 | tf_op jit(solution)/shard_map/all_gather | solution.py:61
  104.3 0.9 add_convert_fusion
  (111 shorter events, 22.9 us)
Async XLA Ops:
  0.0 13.7 %copy-start = (bf16[2,8,64,256]{3,2,1,0:T(8,128)(2,1)S(1)}, bf16[2,8,64,256]{3,2,1,0:T(8,128)(2,1)}, u32[]{:S(2)}) copy-start(bf16[2,8,64,256]{3,2,1,0:T(8,128)(2,1)} %param.5) | copy-start | bytes 1572868
  0.0 18.3 %copy-start.3 = (bf16[3,3,3,256,256]{4,3,2,1,0:T(8,128)(2,1)S(1)}, bf16[3,3,3,256,256]{4,3,2,1,0:T(8,128)(2,1)}, u32[]{:S(2)}) copy-start(bf16[3,3,3,256,256]{4,3,2,1,0:T(8,128)(2,1)} %param.6) | copy-start | bytes 10616836
  1.2 7.1 %collective-permute-start = (bf16[1,8,64,256]{3,2,1,0:T(8,128)(2,1)S(1)}, bf16[1,8,64,256]{3,2,1,0:T(8,128)(2,1)S(1)}, u32[]{:S(2)}, u32[]{:S(2)}) collective-permute-start(bf16[1,8,64,256]{3,2,1,0:T(8,128)(2,1)S(1)} %get-tuple-element.94), channel_id=1, source_target_pairs={{0,2},{2,4},{4,6},{6,8},{8,10},{10,12},{12,14},{14,16},{16,18},{18... | collective-permute-start | bytes 786440 | tf_op jit(solution)/shard_map/ppermute | solution.py:12
  5.1 8.6 %collective-permute-start.1 = (bf16[1,8,64,256]{3,2,1,0:T(8,128)(2,1)S(1)}, bf16[1,8,64,256]{3,2,1,0:T(8,128)(2,1)S(1)}, u32[]{:S(2)}, u32[]{:S(2)}) collective-permute-start(bf16[1,8,64,256]{3,2,1,0:T(8,128)(2,1)S(1)} %get-tuple-element.93), channel_id=1, source_target_pairs={{2,0},{4,2},{6,4},{8,6},{10,8},{12,10},{14,12},{16,14},{18,16},{20... | collective-permute-start | bytes 786440 | tf_op jit(solution)/shard_map/ppermute | solution.py:15
  13.9 5.1 %collective-permute-start.2 = (bf16[4,1,64,256]{3,2,1,0:T(8,128)(2,1)S(1)}, bf16[4,1,64,256]{3,2,1,0:T(8,128)(2,1)S(1)}, u32[]{:S(2)}, u32[]{:S(2)}) collective-permute-start(bf16[4,1,64,256]{3,2,1,0:T(8,128)(2,1)S(1)} %get-tuple-element.60), channel_id=1, source_target_pairs={{0,1},{2,3},{4,5},{6,7},{8,9},{10,11},{12,13},{14,15},{16,17},{18,... | collective-permute-start | bytes 393224 | tf_op jit(solution)/shard_map/ppermute | solution.py:12
  17.0 5.7 %collective-permute-start.3 = (bf16[4,1,64,256]{3,2,1,0:T(8,128)(2,1)S(1)}, bf16[4,1,64,256]{3,2,1,0:T(8,128)(2,1)S(1)}, u32[]{:S(2)}, u32[]{:S(2)}) collective-permute-start(bf16[4,1,64,256]{3,2,1,0:T(8,128)(2,1)S(1)} %get-tuple-element.61), channel_id=1, source_target_pairs={{1,0},{3,2},{5,4},{7,6},{9,8},{11,10},{13,12},{15,14},{17,16},{19,... | collective-permute-start | bytes 393224 | tf_op jit(solution)/shard_map/ppermute | solution.py:15
  37.4 13.3 %copy-start.1 = (bf16[3,3,3,256,256]{4,3,2,1,0:T(8,128)(2,1)S(1)}, bf16[3,3,3,256,256]{4,3,2,1,0:T(8,128)(2,1)}, u32[]{:S(2)}) copy-start(bf16[3,3,3,256,256]{4,3,2,1,0:T(8,128)(2,1)} %param.7) | copy-start | bytes 10616836
  37.5 7.8 %collective-permute-start.4 = (bf16[1,8,64,256]{3,2,1,0:T(8,128)(2,1)S(1)}, bf16[1,8,64,256]{3,2,1,0:T(8,128)(2,1)S(1)}, u32[]{:S(2)}, u32[]{:S(2)}) collective-permute-start(bf16[1,8,64,256]{3,2,1,0:T(8,128)(2,1)S(1)} %bitcast.513), channel_id=1, source_target_pairs={{0,2},{2,4},{4,6},{6,8},{8,10},{10,12},{12,14},{14,16},{16,18},{18... | collective-permute-start | bytes 786440 | tf_op jit(solution)/shard_map/ppermute | solution.py:12
  42.0 8.6 %collective-permute-start.5 = (bf16[1,8,64,256]{3,2,1,0:T(8,128)(2,1)S(1)}, bf16[1,8,64,256]{3,2,1,0:T(8,128)(2,1)S(1)}, u32[]{:S(2)}, u32[]{:S(2)}) collective-permute-start(bf16[1,8,64,256]{3,2,1,0:T(8,128)(2,1)S(1)} %bitcast.512), channel_id=1, source_target_pairs={{2,0},{4,2},{6,4},{8,6},{10,8},{12,10},{14,12},{16,14},{18,16},{20... | collective-permute-start | bytes 786440 | tf_op jit(solution)/shard_map/ppermute | solution.py:15
  51.0 3.2 %collective-permute-start.6 = (bf16[4,1,64,256]{3,2,1,0:T(8,128)(2,1)S(1)}, bf16[4,1,64,256]{3,2,1,0:T(8,128)(2,1)S(1)}, u32[]{:S(2)}, u32[]{:S(2)}) collective-permute-start(bf16[4,1,64,256]{3,2,1,0:T(8,128)(2,1)S(1)} %get-tuple-element.55), channel_id=1, source_target_pairs={{0,1},{2,3},{4,5},{6,7},{8,9},{10,11},{12,13},{14,15},{16,17},{18,... | collective-permute-start | bytes 393224 | tf_op jit(solution)/shard_map/ppermute | solution.py:12
  52.3 5.7 %collective-permute-start.7 = (bf16[4,1,64,256]{3,2,1,0:T(8,128)(2,1)S(1)}, bf16[4,1,64,256]{3,2,1,0:T(8,128)(2,1)S(1)}, u32[]{:S(2)}, u32[]{:S(2)}) collective-permute-start(bf16[4,1,64,256]{3,2,1,0:T(8,128)(2,1)S(1)} %get-tuple-element.56), channel_id=1, source_target_pairs={{1,0},{3,2},{5,4},{7,6},{9,8},{11,10},{13,12},{15,14},{17,16},{19,... | collective-permute-start | bytes 393224 | tf_op jit(solution)/shard_map/ppermute | solution.py:15
  75.9 13.3 %copy-start.2 = (bf16[3,3,3,256,256]{4,3,2,1,0:T(8,128)(2,1)S(1)}, bf16[3,3,3,256,256]{4,3,2,1,0:T(8,128)(2,1)}, u32[]{:S(2)}) copy-start(bf16[3,3,3,256,256]{4,3,2,1,0:T(8,128)(2,1)} %param.8) | copy-start | bytes 10616836
  75.9 7.3 %collective-permute-start.8 = (bf16[1,8,32,256]{3,2,1,0:T(8,128)(2,1)S(1)}, bf16[1,8,32,256]{3,2,1,0:T(8,128)(2,1)S(1)}, u32[]{:S(2)}, u32[]{:S(2)}) collective-permute-start(bf16[1,8,32,256]{3,2,1,0:T(8,128)(2,1)S(1)} %bitcast.479), channel_id=1, source_target_pairs={{0,2},{2,4},{4,6},{6,8},{8,10},{10,12},{12,14},{14,16},{16,18},{18... | collective-permute-start | bytes 393224 | tf_op jit(solution)/shard_map/ppermute | solution.py:12
  81.3 7.2 %collective-permute-start.9 = (bf16[1,8,32,256]{3,2,1,0:T(8,128)(2,1)S(1)}, bf16[1,8,32,256]{3,2,1,0:T(8,128)(2,1)S(1)}, u32[]{:S(2)}, u32[]{:S(2)}) collective-permute-start(bf16[1,8,32,256]{3,2,1,0:T(8,128)(2,1)S(1)} %bitcast.480), channel_id=1, source_target_pairs={{2,0},{4,2},{6,4},{8,6},{10,8},{12,10},{14,12},{16,14},{18,16},{20... | collective-permute-start | bytes 393224 | tf_op jit(solution)/shard_map/ppermute | solution.py:15
  92.9 5.6 %copy-start.4 = (bf16[256,256]{1,0:T(8,128)(2,1)S(1)}, bf16[256,256]{1,0:T(8,128)(2,1)}, u32[]{:S(2)}) copy-start(bf16[256,256]{1,0:T(8,128)(2,1)} %param.9) | copy-start | bytes 393220
  95.1 8.1 %all-to-all-start = ((bf16[1,8,32,256]{3,2,0,1:T(8,128)(2,1)}), bf16[1,8,32,256]{3,2,0,1:T(8,128)(2,1)S(1)}, u32[]{:S(2)}, u32[]{:S(2)}) async-start(bf16[1,8,32,256]{3,2,0,1:T(8,128)(2,1)} %bitcast.167), calls=%async_computation | async-start | bytes 262144 | tf_op jit(solution)/shard_map/all_to_all | solution.py:60
where the time goes:
time: 106 us; the launch traced here: 105 us
  starting transfers between devices  30 us (28%)
  matrix products  27.9 us (26%)
  waiting for transfers between devices  23.7 us (22%)
  local copies, waits for them, and re-layouts  10.1 us (10%)
  blocking collectives  8.73 us (8%)
  other arithmetic  4.03 us (4%)
    dot_general x81, matrix products, convolve(): jnp.dot(window, weight[offset_x, offset_y, offset_z], preferred_element_t...  27.7 us
    ppermute x5, waiting for transfers between devices, extended(): lax.ppermute(lax.slice_in_dim(block, 0, width, axis=dim), axis, backward)  23.4 us
    ppermute x5, starting transfers between devices, extended(): lax.ppermute(lax.slice_in_dim(block, block.shape[dim] - width, None, axis...  18.1 us
    ppermute x5, starting transfers between devices, extended(): lax.ppermute(lax.slice_in_dim(block, 0, width, axis=dim), axis, backward)  8.53 us
    slice x5, local copies, waits for them, and re-layouts, convolve(): padded[offset_x:offset_x + rows_x, offset_y:offset_y + rows_y, offset_z:o...  7.32 us
    all_gather x1, blocking collectives, shards(): whole_projection = lax.all_gather(projection, 'chan', axis=0, tiled=True)  4.7 us
    all_gather x1, blocking collectives, shards(): brick_cells = lax.all_gather(pooled, 'chan', axis=1, tiled=True)  4.03 us
    all_to_all x1, starting transfers between devices, shards(): lax.all_to_all(coarse, 'chan', split_axis=1, concat_axis=3, tiled=True)  3.38 us
  transfers between devices with their start and end apart: 11, of which 7 were waited for; matrix products, arithmetic and copies ran while one was open for 3% of the time, Pallas kernels for 0%

commit v1 on v0

--- a/solution.py
+++ b/solution.py
@@ -58,7 +58,8 @@
     padded = jnp.pad(padded, ((0, 0), (1, 1), (1, 1), (0, 0)))
     coarse = jnp.maximum(convolve(padded, coarse_weight), 0.0).astype(jnp.bfloat16)
     own_cells = lax.all_to_all(coarse, "chan", split_axis=1, concat_axis=3, tiled=True)
-    whole_projection = lax.all_gather(projection, "chan", axis=0, tiled=True)
+    sent = jnp.stack([projection] * lax.axis_size("chan"))
+    whole_projection = jnp.concatenate(lax.all_to_all(sent, "chan", 0, 0), axis=0)
     own_shape = own_cells.shape
     lifted = jnp.dot(
         own_cells.reshape(-1, own_shape[3]), whole_projection, preferred_element_type=jnp.float32

time: 106 us -> 112 us (1.057)
  waiting for transfers between devices: 23.7 us -> 30.1 us
  blocking collectives: 8.73 us -> 4.05 us
  starting transfers between devices: 30 us -> 33.4 us
    all_gather x1 -> x0, blocking collectives: 4.7 us -> none  [shards(): whole_projection = lax.all_gather(projection, 'chan', axis=0, tiled=True)]
    all_to_all x0 -> x1, waiting for transfers between devices: none -> 3.77 us  [shards(): lax.all_to_all(sent, 'chan', 0, 0)]
    all_to_all x0 -> x1, starting transfers between devices: none -> 3.44 us  [shards(): lax.all_to_all(sent, 'chan', 0, 0)]
    all_to_all x1, waiting for transfers between devices: 0.01 us -> 2.58 us  [shards(): lax.all_to_all(coarse, 'chan', split_axis=1, concat_axis=3, tiled=True)]
  transfers between devices with their start and end apart: 11 -> 12, of which waited for: 7 -> 9; matrix products, arithmetic and copies ran while one was open for 3% -> 4% of each run, Pallas kernels for 0% -> 0%
where the time goes in v1:
time: 112 us; the launch traced here: 111 us
  starting transfers between devices  33.4 us (30%)
  waiting for transfers between devices  30.1 us (27%)
  matrix products  27.9 us (25%)
  local copies, waits for them, and re-layouts  10.1 us (9%)
  other arithmetic  4.76 us (4%)
  blocking collectives  4.05 us (4%)
    dot_general x81, matrix products, convolve(): jnp.dot(window, weight[offset_x, offset_y, offset_z], preferred_element_t...  27.7 us
    ppermute x5, waiting for transfers between devices, extended(): lax.ppermute(lax.slice_in_dim(block, 0, width, axis=dim), axis, backward)  23.4 us
    ppermute x5, starting transfers between devices, extended(): lax.ppermute(lax.slice_in_dim(block, block.shape[dim] - width, None, axis...  18.1 us
    ppermute x5, starting transfers between devices, extended(): lax.ppermute(lax.slice_in_dim(block, 0, width, axis=dim), axis, backward)  8.53 us
    slice x5, local copies, waits for them, and re-layouts, convolve(): padded[offset_x:offset_x + rows_x, offset_y:offset_y + rows_y, offset_z:o...  7.32 us
    all_gather x1, blocking collectives, shards(): brick_cells = lax.all_gather(pooled, 'chan', axis=1, tiled=True)  4.05 us
    all_to_all x1, waiting for transfers between devices, shards(): lax.all_to_all(sent, 'chan', 0, 0)  3.77 us
    all_to_all x1, starting transfers between devices, shards(): lax.all_to_all(sent, 'chan', 0, 0)  3.44 us
  transfers between devices with their start and end apart: 12, of which 9 were waited for; matrix products, arithmetic and copies ran while one was open for 4% of the time, Pallas kernels for 0%

profile of v1, /device:TPU:21, one launch (start us, length us, event | category | flops | bytes accessed | tf_op | source)
XLA Modules:
  0.0 111.0 jit_solution(3259697701947125193)
XLA Ops:
  0.0 1.2 %fusion.275 = (bf16[1,8,64,256]{3,2,1,0:T(8,128)(2,1)S(1)}, bf16[1,8,64,256]{3,2,1,0:T(8,128)(2,1)S(1)}) fusion(bf16[2,8,64,256]{3,2,1,0:T(8,128)(2,1)} %param.5), kind=kLoop, calls=%fused_computation.342 | loop fusion | bytes 1048576 | tf_op jit(solution)/shard_map/slice | solution.py:15
  1.2 3.8 %collective-permute-start = (bf16[1,8,64,256]{3,2,1,0:T(8,128)(2,1)S(1)}, bf16[1,8,64,256]{3,2,1,0:T(8,128)(2,1)S(1)}, u32[]{:S(2)}, u32[]{:S(2)}) collective-permute-start(bf16[1,8,64,256]{3,2,1,0:T(8,128)(2,1)S(1)} %get-tuple-element.94), channel_id=1, source_target_pairs={{0,2},{2,4},{4,6},{6,8},{8,10},{10,12},{12,14},{14,16},{16,18},{18... | collective-permute-start | bytes 786440 | tf_op jit(solution)/shard_map/ppermute | solution.py:12
  5.1 1.9 %collective-permute-start.1 = (bf16[1,8,64,256]{3,2,1,0:T(8,128)(2,1)S(1)}, bf16[1,8,64,256]{3,2,1,0:T(8,128)(2,1)S(1)}, u32[]{:S(2)}, u32[]{:S(2)}) collective-permute-start(bf16[1,8,64,256]{3,2,1,0:T(8,128)(2,1)S(1)} %get-tuple-element.93), channel_id=1, source_target_pairs={{2,0},{4,2},{6,4},{8,6},{10,8},{12,10},{14,12},{16,14},{18,16},{20... | collective-permute-start | bytes 786440 | tf_op jit(solution)/shard_map/ppermute | solution.py:15
  7.0 1.4 %fusion.158 = f32[1024,256]{1,0:T(8,128)S(1)} fusion(bf16[1024,256]{1,0:T(8,128)(2,1)} %bitcast.428, bf16[3,3,3,256,256]{4,3,2,1,0:T(8,128)(2,1)} %param.6), kind=kOutput, calls=%fused_computation.220 | convolution fusion | flops 134217728 | bytes 1703936 | tf_op jit(solution)/shard_map/dot_general | solution.py:36
  8.4 5.3 %collective-permute-done.1 = bf16[1,8,64,256]{3,2,1,0:T(8,128)(2,1)S(1)} collective-permute-done((bf16[1,8,64,256]{3,2,1,0:T(8,128)(2,1)S(1)}, bf16[1,8,64,256]{3,2,1,0:T(8,128)(2,1)S(1)}, u32[]{:S(2)}, u32[]{:S(2)}) %collective-permute-start.1) | collective-permute-done | bytes 262176 | tf_op jit(solution)/shard_map/ppermute | solution.py:15
  13.9 3.1 %collective-permute-start.2 = (bf16[4,1,64,256]{3,2,1,0:T(8,128)(2,1)S(1)}, bf16[4,1,64,256]{3,2,1,0:T(8,128)(2,1)S(1)}, u32[]{:S(2)}, u32[]{:S(2)}) collective-permute-start(bf16[4,1,64,256]{3,2,1,0:T(8,128)(2,1)S(1)} %get-tuple-element.60), channel_id=1, source_target_pairs={{0,1},{2,3},{4,5},{6,7},{8,9},{10,11},{12,13},{14,15},{16,17},{18,... | collective-permute-start | bytes 393224 | tf_op jit(solution)/shard_map/ppermute | solution.py:12
  17.0 1.3 %collective-permute-start.3 = (bf16[4,1,64,256]{3,2,1,0:T(8,128)(2,1)S(1)}, bf16[4,1,64,256]{3,2,1,0:T(8,128)(2,1)S(1)}, u32[]{:S(2)}, u32[]{:S(2)}) collective-permute-start(bf16[4,1,64,256]{3,2,1,0:T(8,128)(2,1)S(1)} %get-tuple-element.61), channel_id=1, source_target_pairs={{1,0},{3,2},{5,4},{7,6},{9,8},{11,10},{13,12},{15,14},{17,16},{19,... | collective-permute-start | bytes 393224 | tf_op jit(solution)/shard_map/ppermute | solution.py:15
  19.0 3.8 %collective-permute-done.3 = bf16[4,1,64,256]{3,2,1,0:T(8,128)(2,1)S(1)} collective-permute-done((bf16[4,1,64,256]{3,2,1,0:T(8,128)(2,1)S(1)}, bf16[4,1,64,256]{3,2,1,0:T(8,128)(2,1)S(1)}, u32[]{:S(2)}, u32[]{:S(2)}) %collective-permute-start.3) | collective-permute-done | bytes 131104 | tf_op jit(solution)/shard_map/ppermute | solution.py:15
  22.8 0.8 fusion.8
  23.5 3.1 %fusion.268 = (bf16[2,8,64,256]{3,2,1,0:T(8,128)(2,1)S(1)}, bf16[2,8,64,256]{3,2,1,0:T(8,128)(2,1)S(1)}, bf16[2,8,64,256]{3,2,1,0:T(8,128)(2,1)S(1)}, bf16[2,8,6...) fusion(bf16[4,10,66,256]{3,2,1,0:T(8,128)(2,1)S(1)} %fusion.8), kind=kLoop, calls=%fused_computation.335 | loop fusion | bytes 18874368 | tf_op jit(solution)/shard_map/slice | solution.py:30
  33.5 1.3 %fusion.182 = f32[1024,256]{1,0:T(8,128)} fusion(bf16[1024,256]{1,0:T(8,128)(2,1)S(1)} %bitcast.468, bf16[3,3,3,256,256]{4,3,2,1,0:T(8,128)(2,1)S(1)} %copy-done.3), kind=kOutput, calls=%fused_computation.244 | convolution fusion | flops 134217728 | bytes 1703936 | tf_op jit(solution)/shard_map/dot_general | solution.py:36
  34.8 2.6 %fusion.40 = bf16[1024,256]{1,0:T(8,128)(2,1)S(1)} fusion(f32[1024,256]{1,0:T(8,128)S(1)} %fusion.133, f32[1024,256]{1,0:T(8,128)S(1)} %fusion.135, f32[1024,256]{1,0:T(8,128)S(1)} %fusion.137, f32[1024,256]{1,0:T(8,128)S(1)} %fusion.139, f32[1024,256]{1,0:T(8,128)S(1)} %fusion.141, f32[1024,256]{1,0:T(8,128)S(1)} %fusion.143, ...), kind=kOutput, calls=%fused_computation.59 | convolution fusion | flops 141557760 | bytes 28442624 | tf_op jit(solution)/shard_map/dot_general | solution.py:36
  37.5 4.5 %collective-permute-start.4 = (bf16[1,8,64,256]{3,2,1,0:T(8,128)(2,1)S(1)}, bf16[1,8,64,256]{3,2,1,0:T(8,128)(2,1)S(1)}, u32[]{:S(2)}, u32[]{:S(2)}) collective-permute-start(bf16[1,8,64,256]{3,2,1,0:T(8,128)(2,1)S(1)} %bitcast.516), channel_id=1, source_target_pairs={{0,2},{2,4},{4,6},{6,8},{8,10},{10,12},{12,14},{14,16},{16,18},{18... | collective-permute-start | bytes 786440 | tf_op jit(solution)/shard_map/ppermute | solution.py:12
  42.0 1.9 %collective-permute-start.5 = (bf16[1,8,64,256]{3,2,1,0:T(8,128)(2,1)S(1)}, bf16[1,8,64,256]{3,2,1,0:T(8,128)(2,1)S(1)}, u32[]{:S(2)}, u32[]{:S(2)}) collective-permute-start(bf16[1,8,64,256]{3,2,1,0:T(8,128)(2,1)S(1)} %bitcast.515), channel_id=1, source_target_pairs={{2,0},{4,2},{6,4},{8,6},{10,8},{12,10},{14,12},{16,14},{18,16},{20... | collective-permute-start | bytes 786440 | tf_op jit(solution)/shard_map/ppermute | solution.py:15
  43.9 1.2 %fusion.107 = f32[1024,256]{1,0:T(8,128)S(1)} fusion(bf16[1024,256]{1,0:T(8,128)(2,1)S(1)} %fusion.40, bf16[3,3,3,256,256]{4,3,2,1,0:T(8,128)(2,1)} %param.7), kind=kOutput, calls=%fused_computation.169 | convolution fusion | flops 134217728 | bytes 1703936 | tf_op jit(solution)/shard_map/dot_general | solution.py:36
  45.3 5.3 %collective-permute-done.5 = bf16[1,8,64,256]{3,2,1,0:T(8,128)(2,1)S(1)} collective-permute-done((bf16[1,8,64,256]{3,2,1,0:T(8,128)(2,1)S(1)}, bf16[1,8,64,256]{3,2,1,0:T(8,128)(2,1)S(1)}, u32[]{:S(2)}, u32[]{:S(2)}) %collective-permute-start.5) | collective-permute-done | bytes 262176 | tf_op jit(solution)/shard_map/ppermute | solution.py:15
  51.0 1.3 %collective-permute-start.6 = (bf16[4,1,64,256]{3,2,1,0:T(8,128)(2,1)S(1)}, bf16[4,1,64,256]{3,2,1,0:T(8,128)(2,1)S(1)}, u32[]{:S(2)}, u32[]{:S(2)}) collective-permute-start(bf16[4,1,64,256]{3,2,1,0:T(8,128)(2,1)S(1)} %get-tuple-element.55), channel_id=1, source_target_pairs={{0,1},{2,3},{4,5},{6,7},{8,9},{10,11},{12,13},{14,15},{16,17},{18,... | collective-permute-start | bytes 393224 | tf_op jit(solution)/shard_map/ppermute | solution.py:12
  52.3 1.5 %collective-permute-start.7 = (bf16[4,1,64,256]{3,2,1,0:T(8,128)(2,1)S(1)}, bf16[4,1,64,256]{3,2,1,0:T(8,128)(2,1)S(1)}, u32[]{:S(2)}, u32[]{:S(2)}) collective-permute-start(bf16[4,1,64,256]{3,2,1,0:T(8,128)(2,1)S(1)} %get-tuple-element.56), channel_id=1, source_target_pairs={{1,0},{3,2},{5,4},{7,6},{9,8},{11,10},{13,12},{15,14},{17,16},{19,... | collective-permute-start | bytes 393224 | tf_op jit(solution)/shard_map/ppermute | solution.py:15
  54.3 3.8 %collective-permute-done.7 = bf16[4,1,64,256]{3,2,1,0:T(8,128)(2,1)S(1)} collective-permute-done((bf16[4,1,64,256]{3,2,1,0:T(8,128)(2,1)S(1)}, bf16[4,1,64,256]{3,2,1,0:T(8,128)(2,1)S(1)}, u32[]{:S(2)}, u32[]{:S(2)}) %collective-permute-start.7) | collective-permute-done | bytes 131104 | tf_op jit(solution)/shard_map/ppermute | solution.py:15
  58.1 0.8 select_maximum_fusion
  58.9 3.3 %fusion.267 = (bf16[2,8,64,256]{3,2,1,0:T(8,128)(2,1)S(1)}, bf16[2,8,64,256]{3,2,1,0:T(8,128)(2,1)S(1)}, bf16[2,8,64,256]{3,2,1,0:T(8,128)(2,1)S(1)}, bf16[2,8,6...) fusion(bf16[4,10,66,256]{3,2,1,0:T(8,128)(2,1)S(1)} %select_max, ...), kind=kLoop, calls=%fused_computation.334 | loop fusion | bytes 18874368 | tf_op jit(solution)/shard_map/slice | solution.py:30
  68.1 0.8 fusion.24
  71.9 4.0 %all-gather = bf16[8,32,256]{2,1,0:T(8,128)(2,1)S(1)} all-gather(bf16[4,32,256]{2,1,0:T(8,128)(2,1)S(1)} %multiply_convert_fusion), channel_id=2, replica_groups=mesh['brick'=16,'chan'=2] {'chan'}, dimensions={0}, use_global_device_ids=true | all-gather | bytes 196608 | tf_op jit(solution)/shard_map/all_gather | solution.py:56
  75.9 5.3 %collective-permute-start.8 = (bf16[1,8,32,256]{3,2,1,0:T(8,128)(2,1)S(1)}, bf16[1,8,32,256]{3,2,1,0:T(8,128)(2,1)S(1)}, u32[]{:S(2)}, u32[]{:S(2)}) collective-permute-start(bf16[1,8,32,256]{3,2,1,0:T(8,128)(2,1)S(1)} %bitcast.481), channel_id=1, source_target_pairs={{0,2},{2,4},{4,6},{6,8},{8,10},{10,12},{12,14},{14,16},{16,18},{18... | collective-permute-start | bytes 393224 | tf_op jit(solution)/shard_map/ppermute | solution.py:12
  81.3 1.9 %collective-permute-start.9 = (bf16[1,8,32,256]{3,2,1,0:T(8,128)(2,1)S(1)}, bf16[1,8,32,256]{3,2,1,0:T(8,128)(2,1)S(1)}, u32[]{:S(2)}, u32[]{:S(2)}) collective-permute-start(bf16[1,8,32,256]{3,2,1,0:T(8,128)(2,1)S(1)} %bitcast.482), channel_id=1, source_target_pairs={{2,0},{4,2},{6,4},{8,6},{10,8},{12,10},{14,12},{16,14},{18,16},{20... | collective-permute-start | bytes 393224 | tf_op jit(solution)/shard_map/ppermute | solution.py:15
  83.2 5.2 %collective-permute-done.9 = bf16[1,8,32,256]{3,2,1,0:T(8,128)(2,1)S(1)} collective-permute-done((bf16[1,8,32,256]{3,2,1,0:T(8,128)(2,1)S(1)}, bf16[1,8,32,256]{3,2,1,0:T(8,128)(2,1)S(1)}, u32[]{:S(2)}, u32[]{:S(2)}) %collective-permute-start.9) | collective-permute-done | bytes 131104 | tf_op jit(solution)/shard_map/ppermute | solution.py:15
  94.3 0.8 fusion.47
  95.1 3.4 %all-to-all-start = ((bf16[1,8,32,256]{3,2,0,1:T(8,128)(2,1)}), bf16[1,8,32,256]{3,2,0,1:T(8,128)(2,1)S(1)}, u32[]{:S(2)}, u32[]{:S(2)}) async-start(bf16[1,8,32,256]{3,2,0,1:T(8,128)(2,1)} %bitcast.167), calls=%async_computation | async-start | bytes 262144 | tf_op jit(solution)/shard_map/all_to_all | solution.py:60
  99.3 2.6 %all-to-all-done = bf16[1,8,32,256]{3,2,0,1:T(8,128)(2,1)S(1)} async-done(((bf16[1,8,32,256]{3,2,0,1:T(8,128)(2,1)}), bf16[1,8,32,256]{3,2,0,1:T(8,128)(2,1)S(1)}, u32[]{:S(2)}, u32[]{:S(2)}) %all-to-all-start) | async-done | bytes 131104 | tf_op jit(solution)/shard_map/all_to_all | solution.py:60
  101.8 3.4 %all-to-all-start.1 = ((bf16[2,256,256]{2,1,0:T(8,128)(2,1)}), bf16[2,256,256]{2,1,0:T(8,128)(2,1)S(1)}, u32[]{:S(2)}, u32[]{:S(2)}) async-start(bf16[2,256,256]{2,1,0:T(8,128)(2,1)} %pad_maximum_fusion.7), calls=%async_computation.1 | async-start | bytes 524288 | tf_op jit(solution)/shard_map/all_to_all | solution.py:62
  105.5 3.8 %all-to-all-done.1 = bf16[2,256,256]{2,1,0:T(8,128)(2,1)S(1)} async-done(((bf16[2,256,256]{2,1,0:T(8,128)(2,1)}), bf16[2,256,256]{2,1,0:T(8,128)(2,1)S(1)}, u32[]{:S(2)}, u32[]{:S(2)}) %all-to-all-start.1) | async-done | bytes 262176 | tf_op jit(solution)/shard_map/all_to_all | solution.py:62
  110.1 0.9 add_convert_fusion
  (113 shorter events, 24.9 us)
Async XLA Ops:
  0.0 13.7 %copy-start = (bf16[2,8,64,256]{3,2,1,0:T(8,128)(2,1)S(1)}, bf16[2,8,64,256]{3,2,1,0:T(8,128)(2,1)}, u32[]{:S(2)}) copy-start(bf16[2,8,64,256]{3,2,1,0:T(8,128)(2,1)} %param.5) | copy-start | bytes 1572868
  0.0 18.3 %copy-start.3 = (bf16[3,3,3,256,256]{4,3,2,1,0:T(8,128)(2,1)S(1)}, bf16[3,3,3,256,256]{4,3,2,1,0:T(8,128)(2,1)}, u32[]{:S(2)}) copy-start(bf16[3,3,3,256,256]{4,3,2,1,0:T(8,128)(2,1)} %param.6) | copy-start | bytes 10616836
  1.2 7.1 %collective-permute-start = (bf16[1,8,64,256]{3,2,1,0:T(8,128)(2,1)S(1)}, bf16[1,8,64,256]{3,2,1,0:T(8,128)(2,1)S(1)}, u32[]{:S(2)}, u32[]{:S(2)}) collective-permute-start(bf16[1,8,64,256]{3,2,1,0:T(8,128)(2,1)S(1)} %get-tuple-element.94), channel_id=1, source_target_pairs={{0,2},{2,4},{4,6},{6,8},{8,10},{10,12},{12,14},{14,16},{16,18},{18... | collective-permute-start | bytes 786440 | tf_op jit(solution)/shard_map/ppermute | solution.py:12
  5.1 8.6 %collective-permute-start.1 = (bf16[1,8,64,256]{3,2,1,0:T(8,128)(2,1)S(1)}, bf16[1,8,64,256]{3,2,1,0:T(8,128)(2,1)S(1)}, u32[]{:S(2)}, u32[]{:S(2)}) collective-permute-start(bf16[1,8,64,256]{3,2,1,0:T(8,128)(2,1)S(1)} %get-tuple-element.93), channel_id=1, source_target_pairs={{2,0},{4,2},{6,4},{8,6},{10,8},{12,10},{14,12},{16,14},{18,16},{20... | collective-permute-start | bytes 786440 | tf_op jit(solution)/shard_map/ppermute | solution.py:15
  13.9 5.1 %collective-permute-start.2 = (bf16[4,1,64,256]{3,2,1,0:T(8,128)(2,1)S(1)}, bf16[4,1,64,256]{3,2,1,0:T(8,128)(2,1)S(1)}, u32[]{:S(2)}, u32[]{:S(2)}) collective-permute-start(bf16[4,1,64,256]{3,2,1,0:T(8,128)(2,1)S(1)} %get-tuple-element.60), channel_id=1, source_target_pairs={{0,1},{2,3},{4,5},{6,7},{8,9},{10,11},{12,13},{14,15},{16,17},{18,... | collective-permute-start | bytes 393224 | tf_op jit(solution)/shard_map/ppermute | solution.py:12
  17.0 5.7 %collective-permute-start.3 = (bf16[4,1,64,256]{3,2,1,0:T(8,128)(2,1)S(1)}, bf16[4,1,64,256]{3,2,1,0:T(8,128)(2,1)S(1)}, u32[]{:S(2)}, u32[]{:S(2)}) collective-permute-start(bf16[4,1,64,256]{3,2,1,0:T(8,128)(2,1)S(1)} %get-tuple-element.61), channel_id=1, source_target_pairs={{1,0},{3,2},{5,4},{7,6},{9,8},{11,10},{13,12},{15,14},{17,16},{19,... | collective-permute-start | bytes 393224 | tf_op jit(solution)/shard_map/ppermute | solution.py:15
  37.4 13.3 %copy-start.1 = (bf16[3,3,3,256,256]{4,3,2,1,0:T(8,128)(2,1)S(1)}, bf16[3,3,3,256,256]{4,3,2,1,0:T(8,128)(2,1)}, u32[]{:S(2)}) copy-start(bf16[3,3,3,256,256]{4,3,2,1,0:T(8,128)(2,1)} %param.7) | copy-start | bytes 10616836
  37.5 7.8 %collective-permute-start.4 = (bf16[1,8,64,256]{3,2,1,0:T(8,128)(2,1)S(1)}, bf16[1,8,64,256]{3,2,1,0:T(8,128)(2,1)S(1)}, u32[]{:S(2)}, u32[]{:S(2)}) collective-permute-start(bf16[1,8,64,256]{3,2,1,0:T(8,128)(2,1)S(1)} %bitcast.516), channel_id=1, source_target_pairs={{0,2},{2,4},{4,6},{6,8},{8,10},{10,12},{12,14},{14,16},{16,18},{18... | collective-permute-start | bytes 786440 | tf_op jit(solution)/shard_map/ppermute | solution.py:12
  42.0 8.6 %collective-permute-start.5 = (bf16[1,8,64,256]{3,2,1,0:T(8,128)(2,1)S(1)}, bf16[1,8,64,256]{3,2,1,0:T(8,128)(2,1)S(1)}, u32[]{:S(2)}, u32[]{:S(2)}) collective-permute-start(bf16[1,8,64,256]{3,2,1,0:T(8,128)(2,1)S(1)} %bitcast.515), channel_id=1, source_target_pairs={{2,0},{4,2},{6,4},{8,6},{10,8},{12,10},{14,12},{16,14},{18,16},{20... | collective-permute-start | bytes 786440 | tf_op jit(solution)/shard_map/ppermute | solution.py:15
  51.0 3.2 %collective-permute-start.6 = (bf16[4,1,64,256]{3,2,1,0:T(8,128)(2,1)S(1)}, bf16[4,1,64,256]{3,2,1,0:T(8,128)(2,1)S(1)}, u32[]{:S(2)}, u32[]{:S(2)}) collective-permute-start(bf16[4,1,64,256]{3,2,1,0:T(8,128)(2,1)S(1)} %get-tuple-element.55), channel_id=1, source_target_pairs={{0,1},{2,3},{4,5},{6,7},{8,9},{10,11},{12,13},{14,15},{16,17},{18,... | collective-permute-start | bytes 393224 | tf_op jit(solution)/shard_map/ppermute | solution.py:12
  52.3 5.7 %collective-permute-start.7 = (bf16[4,1,64,256]{3,2,1,0:T(8,128)(2,1)S(1)}, bf16[4,1,64,256]{3,2,1,0:T(8,128)(2,1)S(1)}, u32[]{:S(2)}, u32[]{:S(2)}) collective-permute-start(bf16[4,1,64,256]{3,2,1,0:T(8,128)(2,1)S(1)} %get-tuple-element.56), channel_id=1, source_target_pairs={{1,0},{3,2},{5,4},{7,6},{9,8},{11,10},{13,12},{15,14},{17,16},{19,... | collective-permute-start | bytes 393224 | tf_op jit(solution)/shard_map/ppermute | solution.py:15
  75.9 13.3 %copy-start.2 = (bf16[3,3,3,256,256]{4,3,2,1,0:T(8,128)(2,1)S(1)}, bf16[3,3,3,256,256]{4,3,2,1,0:T(8,128)(2,1)}, u32[]{:S(2)}) copy-start(bf16[3,3,3,256,256]{4,3,2,1,0:T(8,128)(2,1)} %param.8) | copy-start | bytes 10616836
  75.9 7.3 %collective-permute-start.8 = (bf16[1,8,32,256]{3,2,1,0:T(8,128)(2,1)S(1)}, bf16[1,8,32,256]{3,2,1,0:T(8,128)(2,1)S(1)}, u32[]{:S(2)}, u32[]{:S(2)}) collective-permute-start(bf16[1,8,32,256]{3,2,1,0:T(8,128)(2,1)S(1)} %bitcast.481), channel_id=1, source_target_pairs={{0,2},{2,4},{4,6},{6,8},{8,10},{10,12},{12,14},{14,16},{16,18},{18... | collective-permute-start | bytes 393224 | tf_op jit(solution)/shard_map/ppermute | solution.py:12
  81.3 7.2 %collective-permute-start.9 = (bf16[1,8,32,256]{3,2,1,0:T(8,128)(2,1)S(1)}, bf16[1,8,32,256]{3,2,1,0:T(8,128)(2,1)S(1)}, u32[]{:S(2)}, u32[]{:S(2)}) collective-permute-start(bf16[1,8,32,256]{3,2,1,0:T(8,128)(2,1)S(1)} %bitcast.482), channel_id=1, source_target_pairs={{2,0},{4,2},{6,4},{8,6},{10,8},{12,10},{14,12},{16,14},{18,16},{20... | collective-permute-start | bytes 393224 | tf_op jit(solution)/shard_map/ppermute | solution.py:15
  92.9 5.6 %copy-start.4 = (bf16[256,256]{1,0:T(8,128)(2,1)S(1)}, bf16[256,256]{1,0:T(8,128)(2,1)}, u32[]{:S(2)}) copy-start(bf16[256,256]{1,0:T(8,128)(2,1)} %param.9) | copy-start | bytes 393220
  95.1 6.7 %all-to-all-start = ((bf16[1,8,32,256]{3,2,0,1:T(8,128)(2,1)}), bf16[1,8,32,256]{3,2,0,1:T(8,128)(2,1)S(1)}, u32[]{:S(2)}, u32[]{:S(2)}) async-start(bf16[1,8,32,256]{3,2,0,1:T(8,128)(2,1)} %bitcast.167), calls=%async_computation | async-start | bytes 262144 | tf_op jit(solution)/shard_map/all_to_all | solution.py:60
  101.8 7.5 %all-to-all-start.1 = ((bf16[2,256,256]{2,1,0:T(8,128)(2,1)}), bf16[2,256,256]{2,1,0:T(8,128)(2,1)S(1)}, u32[]{:S(2)}, u32[]{:S(2)}) async-start(bf16[2,256,256]{2,1,0:T(8,128)(2,1)} %pad_maximum_fusion.7), calls=%async_computation.1 | async-start | bytes 524288 | tf_op jit(solution)/shard_map/all_to_all | solution.py:62
